TPU v7x, 8 devices: a whole 2x2x1 slice. The times are simulated.
8 devices in a mesh: dp: 1 (over z), tp: 8 (over y, x, core).
Axes of the slice: x: 2, y: 2, z: 1, core: 2. Of those that a mesh axis runs over, the one named last changes fastest.
Arguments:
- x_a: bfloat16 [4096, 4096], P(('dp', 'tp'))
- x_b: bfloat16 [4096, 4096], P(('dp', 'tp'))
- labels_a: int32 [4096], P(('dp', 'tp'))
- labels_b: int32 [4096], P(('dp', 'tp'))
- w_head: bfloat16 [4096, 32768], P(None, 'tp')
Outputs:
- output 1: float32 [2], P('dp')
- output 2: bfloat16 [4096, 32768], P('dp', 'tp')
- output 3: bfloat16 [4096, 4096], P(('dp', 'tp'))
- output 4: bfloat16 [4096, 4096], P(('dp', 'tp'))
All inputs are finite; a program needn't handle non-finite values.
Results may differ from a plain program's by a relative error of at most 0.001.
Values are sent between devices in bfloat16 or wider.
A program may use at most 1 GiB of HBM per device.

v0:
```python
import jax
import jax.numpy as jnp
from jax import lax
from jax.sharding import PartitionSpec as P


def solution(mesh):
    group_size = mesh.shape["tp"]

    def local_step(x_a, x_b, labels_a, labels_b, w_local):
        tok_rows = x_a.shape[0]
        shard_cols = w_local.shape[1]
        tokens = tok_rows * group_size
        x_full = lax.all_gather(jnp.stack([x_a, x_b]), "tp", axis=1, tiled=True)
        label_full = lax.all_gather(jnp.stack([labels_a, labels_b]), "tp", axis=1, tiled=True)
        logits = jnp.einsum("mth,hv->mtv", x_full, w_local, preferred_element_type=jnp.float32)
        col_ids = lax.broadcasted_iota(jnp.int32, (1, 1, shard_cols), 2) + lax.axis_index("tp") * shard_cols
        label_hit = col_ids == label_full[..., None]
        local_target = jnp.sum(jnp.where(label_hit, logits, 0.0), axis=-1)
        row_max = lax.pmax(jnp.max(logits, axis=-1), "tp")
        shifted = jnp.exp(logits - row_max[..., None])
        stat_sums = lax.psum(jnp.stack([jnp.sum(shifted, axis=-1), local_target]), "tp")
        row_sum = stat_sums[0]
        loss_tok = row_max + jnp.log(row_sum) - stat_sums[1]
        losses = jnp.mean(loss_tok, axis=-1)
        grad_logits = ((shifted / row_sum[..., None] - label_hit.astype(jnp.float32)) / tokens).astype(jnp.bfloat16)
        grad_w = jnp.einsum("mth,mtv->hv", x_full, grad_logits, preferred_element_type=jnp.float32).astype(jnp.bfloat16)
        grad_part = jnp.einsum("mtv,hv->mth", grad_logits, w_local, preferred_element_type=jnp.float32)
        grad_x = lax.psum_scatter(grad_part, "tp", scatter_dimension=1, tiled=True).astype(jnp.bfloat16)
        return losses, grad_w, grad_x[0], grad_x[1]

    row_spec = P(("dp", "tp"), None)
    label_spec = P(("dp", "tp"))
    return jax.shard_map(local_step, mesh=mesh, in_specs=(row_spec, row_spec, label_spec, label_spec, P(None, "tp")), out_specs=(P("dp"), P("dp", "tp"), row_spec, row_spec), check_vma=False)
```

profile of v0, /device:TPU:0, one launch (start us, length us, event | category | flops | bytes accessed | tf_op | source)
XLA Modules:
  0.0 1829.8 jit_solution(16061764040084428399)
XLA Ops:
  7.2 0.0 all-gather.2.cloned.1.call-start
  7.2 7.6 pad_maximum_fusion
  14.8 0.0 all-gather.2.cloned.1.call-update
  14.9 0.0 all-reduce.2.cloned.1.call-start
  14.9 0.7 pad_add_fusion
  15.6 13.8 all_gather.7
  29.4 0.6 iota_add_fusion
  30.0 285.0 %all-gather.2.cloned.1.call-done = bf16[2,4096,4096]{2,1,0:T(8,128)(2,1)} async-done(((bf16[2,512,4096]{2,1,0:T(8,128)(2,1)}), bf16[2,4096,4096]{2,1,0:T(8,128)(2,1)}) %all-gather.2.cloned.1.call-update) | async-done | bytes 67108880 | tf_op jit(solution)/shard_map/all_gather | solution.py:14
  315.1 0.0 copy-start.2
  315.1 0.0 copy-start.3
  315.1 301.1 %fusion.11 = (f32[2,4096]{1,0:T(2,128)S(1)}, f32[2,4096,4096]{1,2,0:T(8,128)}) fusion(bf16[2,4096,4096]{2,1,0:T(8,128)(2,1)} %all-gather.2.cloned.1.call-done, bf16[4096,4096]{1,0:T(8,128)(2,1)} %param.9), kind=kOutput, calls=%fused_computation.24 | convolution fusion | flops 274911461376 | bytes 234913792 | tf_op jit(solution)/shard_map/mth,hv->mtv/dot_general | solution.py:16
  616.1 22.4 %pmax.7 = f32[2,4096]{1,0:T(2,128)S(1)} all-reduce(f32[2,4096]{1,0:T(2,128)S(1)} %get-tuple-element.8), channel_id=1, replica_groups=mesh['dp'=1,'tp'=8] {'tp'}, use_global_device_ids=true, to_apply=%region_1.2 | all-reduce | flops 8192 | bytes 65536 | tf_op jit(solution)/shard_map/pmax | solution.py:20
  638.5 0.0 copy-start
  638.5 0.0 copy-done.2
  638.5 0.0 copy-done.3
  638.6 41.3 %fusion.4 = (f32[2,4096]{1,0:T(2,128)S(1)}, f32[2,4096]{1,0:T(2,128)S(1)}) fusion(f32[2,4096,4096]{1,2,0:T(8,128)} %get-tuple-element.9, f32[2,4096]{1,0:T(2,128)S(1)} %pmax.7, s32[2,4096]{1,0:T(2,128)S(1)} %copy-done.2, s32[4096]{0:T(1024)S(1)} %copy-done.3), kind=kLoop, calls=%fused_computation.7 | loop fusion | flops 167755776 | bytes 134365184 | tf_op jit(solution)/shard_map/reduce_sum | solution.py:22
  679.9 0.7 pad_maximum_fusion.1
  680.6 0.0 all-reduce.2.cloned.1.call-update
  680.6 0.2 reduce-scatter.2.cloned.1.call-start
  680.8 43.6 %all-reduce.2.cloned.1.call-done = f32[2,2,4096]{2,1,0:T(2,128)} async-done(((f32[2,2,4096]{2,1,0:T(2,128)}), f32[2,2,4096]{2,1,0:T(2,128)}) %all-reduce.2.cloned.1.call-update) | async-done | bytes 65552 | tf_op jit(solution)/shard_map/psum | solution.py:22
  724.4 0.8 slice_bitcast_fusion.3
  725.2 0.0 copy-done
  725.2 64.7 %fusion.3 = bf16[2,4096,4096]{1,2,0:T(8,128)(2,1)} fusion(f32[2,4096,4096]{1,2,0:T(8,128)} %get-tuple-element.9, f32[2,4096]{1,0:T(2,128)S(1)} %slice_bitcast_fusion.3, s32[2,4096]{1,0:T(2,128)S(1)} %copy-done.2, f32[2,4096]{1,0:T(2,128)S(1)} %pmax.7, s32[4096]{0:T(1024)S(1)} %copy-done.3), kind=kLoop, calls=%fused_computation.5 | loop fusion | flops 234881024 | bytes 201441280 | tf_op jit(solution)/shard_map/convert_element_type | solution.py:26
  789.9 291.6 %fusion.5 = f32[2,4096,4096]{2,1,0:T(8,128)} fusion(bf16[2,4096,4096]{1,2,0:T(8,128)(2,1)} %fusion.3, bf16[4096,4096]{1,0:T(8,128)(2,1)} %param.9), kind=kOutput, calls=%fused_computation.9 | convolution fusion | flops 274877906944 | bytes 234881024 | tf_op jit(solution)/shard_map/mtv,hv->mth/dot_general | solution.py:28
  1081.5 0.0 copy-start.1
  1081.5 0.0 copy-start.4
  1081.5 0.0 reduce-scatter.2.cloned.1.call-update
  1081.5 0.7 copy-done.1
  1082.2 0.1 copy-done.4
  1082.3 0.2 fusion.10
  1082.5 0.5 broadcast_multiply_fusion
  1083.0 297.6 %bitcast_convert_fusion = bf16[4096,4096]{1,0:T(8,128)(2,1)} fusion(bf16[2,4096,4096]{2,1,0:T(8,128)(2,1)} %all-gather.2.cloned.1.call-done, bf16[2,4096,4096]{1,2,0:T(8,128)(2,1)} %fusion.3), kind=kOutput, calls=%fused_computation.8 | convolution fusion | flops 274894684160 | bytes 167772160 | tf_op jit(solution)/shard_map/mth,mtv->hv/dot_general | solution.py:27
  1380.6 432.3 %reduce-scatter.2.cloned.1.call-done = f32[2,512,4096]{2,1,0:T(8,128)} async-done(((f32[2,4096,4096]{2,1,0:T(8,128)}), f32[2,512,4096]{2,1,0:T(8,128)}) %reduce-scatter.2.cloned.1.call-update) | async-done | bytes 16777232 | tf_op jit(solution)/shard_map/reduce_scatter | solution.py:29
  1812.9 6.5 convert_element_type.15
  1819.4 3.9 slice_bitcast_fusion
Async XLA Ops:
  7.2 307.9 %all-gather.2.cloned.1.call-start = ((), (), s32[]{:S(2)}) async-start(), calls=%async_computation.1 | async-start | bytes 75497472 | tf_op jit(solution)/shard_map/all_gather | solution.py:14
  14.9 709.6 %all-reduce.2.cloned.1.call-start = ((), (), s32[]{:S(2)}) async-start(), calls=%async_computation.2 | async-start | bytes 131072 | tf_op jit(solution)/shard_map/psum | solution.py:22
  315.1 323.5 %copy-start.2 = (s32[2,4096]{1,0:T(2,128)S(1)}, s32[2,4096]{1,0:T(2,128)}, u32[]{:S(2)}) copy-start(s32[2,4096]{1,0:T(2,128)} %all_gather.7) | copy-start | bytes 98308
  315.1 323.5 %copy-start.3 = (s32[4096]{0:T(1024)S(1)}, s32[4096]{0:T(1024)}, u32[]{:S(2)}) copy-start(s32[4096]{0:T(1024)} %iota_add_fusion) | copy-start | bytes 49156
  638.5 86.7 %copy-start = (f32[2,4096]{1,0:T(2,128)}, f32[2,4096]{1,0:T(2,128)S(1)}, u32[]{:S(2)}) copy-start(f32[2,4096]{1,0:T(2,128)S(1)} %pmax.7) | copy-start | bytes 98308
  680.6 1132.3 %reduce-scatter.2.cloned.1.call-start = ((), (), s32[]{:S(2)}) async-start(), calls=%async_computation.3 | async-start | bytes 150994944 | tf_op jit(solution)/shard_map/reduce_scatter | solution.py:29
  1081.5 0.8 copy-start.1
  1081.5 0.9 copy-start.4
Sparse Core Ops, SparseCore 0:
  15.0 300.0 all-gather.1
  680.7 43.6 all-reduce.1
  1081.6 731.2 reduce-scatter.1
where the time goes:
time: 1830 us
  matrix products  890 us (49%)
  waiting for transfers between devices  761 us (42%)
  other arithmetic  123 us (7%)
  blocking collectives  36.2 us (2%)
    reduce_scatter x1, waiting for transfers between devices, local_step(): lax.psum_scatter(grad_part, 'tp', scatter_dimension=1, tiled=True)  432 us
    dot_general x1, matrix products, local_step(): jnp.einsum('mth,hv->mtv', x_full, w_local, preferred_element_type=jnp.flo...  301 us
    dot_general x1, matrix products, local_step(): jnp.einsum('mth,mtv->hv', x_full, grad_logits, preferred_element_type=jnp...  298 us
    dot_general x1, matrix products, local_step(): jnp.einsum('mtv,hv->mth', grad_logits, w_local, preferred_element_type=jn...  292 us
    all_gather x1, waiting for transfers between devices, local_step(): x_full = lax.all_gather(jnp.stack([x_a, x_b]), 'tp', axis=1, tiled=True)  285 us
    convert_element_type x1, other arithmetic, local_step(): ((shifted / row_sum[..., None] - label_hit.astype(jnp.float32)) / tokens)...  64.7 us
    psum x1, waiting for transfers between devices, local_step(): lax.psum(jnp.stack([jnp.sum(shifted, axis=-1), local_target]), 'tp')  43.6 us
    reduce_sum x1, other arithmetic, local_step(): jnp.sum(shifted, axis=-1)  41.3 us
  transfers between devices with their start and end apart: 3, of which 3 were waited for; matrix products, arithmetic and copies ran while one was open for 16% of the time, Pallas kernels for 0%

commit v1 on v0

v1 whole, which is shorter than its diff:
```python
import functools

import jax
import jax.numpy as jnp
from jax import lax
from jax.experimental import pallas as pl
from jax.experimental.pallas import tpu as pltpu
from jax.sharding import PartitionSpec as P

PIECES = ((0, 128), (0, 128), (0, 256), (1, 256), (1, 256))
LANES = 128


def logits_kernel(cols, x_ref, w_ref, lab_ref, z_ref, m_ref, s_ref, t_ref, m_acc, s_acc, t_acc):
    v = pl.program_id(0)
    rows, tile = x_ref.shape[0], 512

    @pl.when(v == 0)
    def _():
        m_acc[...] = jnp.full_like(m_acc, -jnp.inf)
        s_acc[...] = jnp.zeros_like(s_acc)
        t_acc[...] = jnp.zeros_like(t_acc)

    def fold(start, count):
        sl = pl.ds(start, count)
        lab = lab_ref[sl, :] - v * cols
        parts = [z_ref[sl, k:k + LANES] for k in range(0, cols, LANES)]
        m_old = m_acc[sl, :]
        m_new = functools.reduce(jnp.maximum, parts, m_old)
        total = s_acc[sl, :] * jnp.exp(m_old - m_new)
        target = t_acc[sl, :]
        lane = lax.broadcasted_iota(jnp.int32, (count, LANES), 1)
        for k, part in enumerate(parts):
            total = total + jnp.exp(part - m_new)
            target = target + jnp.where(lane == lab - k * LANES, part, 0.0)
        m_acc[sl, :], s_acc[sl, :], t_acc[sl, :] = m_new, total, target

    for r in range(0, rows + tile, tile):
        if r > 0:
            for q in range(r - tile, r, 64):
                fold(q, 64)
        if r < rows:
            z_ref[r:r + tile, :] = jnp.dot(x_ref[r:r + tile, :], w_ref[...], preferred_element_type=jnp.float32)

    @pl.when(v == pl.num_programs(0) - 1)
    def _():
        m = jnp.max(m_acc[...], axis=1, keepdims=True)
        s = jnp.sum(s_acc[...] * jnp.exp(m_acc[...] - m), axis=1, keepdims=True)
        t = jnp.sum(t_acc[...], axis=1, keepdims=True)
        m_ref[...] = jnp.broadcast_to(m, m_ref.shape)
        s_ref[...] = jnp.broadcast_to(s, s_ref.shape)
        t_ref[...] = jnp.broadcast_to(t, t_ref.shape)


def logits_call(x, w, lab, cols=512):
    rows, hidden = x.shape
    vocab = w.shape[1]
    stat = jax.ShapeDtypeStruct((rows, LANES), jnp.float32)
    stat_spec = pl.BlockSpec((rows, LANES), lambda v: (0, 0))
    return pl.pallas_call(
        functools.partial(logits_kernel, cols), name="logits",
        grid=(vocab // cols,),
        in_specs=[pl.BlockSpec((rows, hidden), lambda v: (0, 0)), pl.BlockSpec((hidden, cols), lambda v: (0, v)), pl.BlockSpec((rows, 1), lambda v: (0, 0))],
        out_specs=[pl.BlockSpec((rows, cols), lambda v: (0, v)), stat_spec, stat_spec, stat_spec],
        out_shape=[jax.ShapeDtypeStruct((rows, vocab), jnp.float32), stat, stat, stat],
        scratch_shapes=[pltpu.VMEM((rows, LANES), jnp.float32)] * 3,
        compiler_params=pltpu.CompilerParams(vmem_limit_bytes=63 << 20, dimension_semantics=("arbitrary",)),
        cost_estimate=pl.CostEstimate(flops=2 * rows * hidden * vocab, bytes_accessed=(rows + vocab) * hidden * 2 + rows * vocab * 4, transcendentals=rows * vocab),
    )(x, w, lab)


def wgrad_kernel(count, *refs):
    total = None
    for x_ref, g_ref in zip(refs[:count], refs[count:2 * count]):
        part = lax.dot_general(x_ref[...], g_ref[...], (((0,), (0,)), ((), ())), preferred_element_type=jnp.float32)
        total = part if total is None else total + part
    refs[-1][...] = total.astype(refs[-1].dtype)


def wgrad_call(xs, gs, bh=512, bv=1024):
    hidden, vocab, rows = xs[0].shape[1], gs[0].shape[1], sum(x.shape[0] for x in xs)
    return pl.pallas_call(
        functools.partial(wgrad_kernel, len(xs)), name="wgrad",
        grid=(vocab // bv, hidden // bh),
        in_specs=[pl.BlockSpec((x.shape[0], bh), lambda v, h: (0, h)) for x in xs] + [pl.BlockSpec((g.shape[0], bv), lambda v, h: (0, v)) for g in gs],
        out_specs=pl.BlockSpec((bh, bv), lambda v, h: (h, v)),
        out_shape=jax.ShapeDtypeStruct((hidden, vocab), jnp.bfloat16),
        compiler_params=pltpu.CompilerParams(vmem_limit_bytes=63 << 20, dimension_semantics=("arbitrary", "arbitrary")),
        cost_estimate=pl.CostEstimate(flops=2 * rows * hidden * vocab, bytes_accessed=rows * (hidden + vocab) * 2 + hidden * vocab * 2, transcendentals=0),
    )(*xs, *gs)


def after(value, token):
    return lax.optimization_barrier((value, token))[0]


def solution(mesh):
    n = mesh.shape["tp"]

    def local_step(x_a, x_b, labels_a, labels_b, w):
        tokens = x_a.shape[0] * n
        cols = w.shape[1]
        me = lax.axis_index("tp")
        xs = (x_a, x_b)
        labels = lax.all_gather(jnp.stack([labels_a, labels_b]), "tp", axis=0, tiled=False) - me * cols
        col_ids = lax.broadcasted_iota(jnp.int32, (1, cols), 1)
        starts, fill = [], [0, 0]
        for mb, size in PIECES:
            starts.append(fill[mb])
            fill[mb] += size

        def gather(i, token=None):
            mb, size = PIECES[i]
            x = xs[mb][starts[i]:starts[i] + size]
            x = x if token is None else after(x, token)
            return lax.all_gather(x, "tp", axis=0, tiled=True)

        labs = [labels[:, mb, s0:s0 + size].reshape(-1, 1) for (mb, size), s0 in zip(PIECES, starts)]

        def forward(i, x, token=None):
            x = x if token is None else after(x, token)
            z, m, s, t = logits_call(x, w, labs[i])
            return z, jnp.stack([m[:, 0], s[:, 0], t[:, 0]])

        def combine(parts):
            every = lax.all_gather(jnp.concatenate(parts, axis=1), "tp", axis=0, tiled=False)
            m_all, s_all, t_all = every[:, 0], every[:, 1], every[:, 2]
            m = jnp.max(m_all, axis=0)
            s = jnp.sum(s_all * jnp.exp(m_all - m), axis=0)
            return m, s, jnp.mean(m + jnp.log(s) - jnp.sum(t_all, axis=0))

        def backward(i, z, stat, token):
            z = after(z, token)
            lo, hi = starts[i] * n, (starts[i] + PIECES[i][1]) * n
            m, s = stat[0][lo:hi, None], stat[1][lo:hi, None]
            hit = (col_ids == labs[i]).astype(jnp.float32)
            g = ((jnp.exp(z - m) / s - hit) / tokens).astype(jnp.bfloat16)
            g = lax.optimization_barrier(g)
            part = lax.dot_general(g, w, (((1,), (1,)), ((), ())), preferred_element_type=jnp.float32)
            return g, part, lax.psum_scatter(part, "tp", scatter_dimension=0, tiled=True)

        gx = [gather(i) for i in range(5)]
        z0, st0 = forward(0, gx[0])
        z1, st1 = forward(1, gx[1], z0)
        z2, st2 = forward(2, gx[2], z1)
        stat_a = combine([st0, st1, st2])
        b0 = backward(0, z0, stat_a, z2)
        b1 = backward(1, z1, stat_a, (b0[1], gx[3], gx[4]))
        b2 = backward(2, z2, stat_a, b1[1])
        z3, st3 = forward(3, gx[3], b2[1])
        z4, st4 = forward(4, gx[4], (z3, b0[2]))
        stat_b = combine([st3, st4])
        b3 = backward(3, z3, stat_b, (z4, b1[2]))
        b4 = backward(4, z4, stat_b, b3[1])
        b = [b0, b1, b2, b3, b4]
        grad_w = wgrad_call(gx, [b0[0], b1[0], b2[0], b3[0], after(b4[0], b4[1])])
        dx = [v[2].astype(jnp.bfloat16) for v in b]
        losses = jnp.stack([stat_a[2], stat_b[2]])
        return losses, grad_w, jnp.concatenate(dx[:3]), jnp.concatenate(dx[3:])

    row_spec = P(("dp", "tp"), None)
    label_spec = P(("dp", "tp"))
    return jax.shard_map(local_step, mesh=mesh, in_specs=(row_spec, row_spec, label_spec, label_spec, P(None, "tp")), out_specs=(P("dp"), P("dp", "tp"), row_spec, row_spec), check_vma=False)
```

time: 1830 us -> 1270 us (0.69)
  waiting for transfers between devices: 761 us -> 74.5 us
  Pallas kernels: 0 us -> 653 us
  matrix products: 890 us -> 322 us
  local copies, waits for them, and re-layouts: 5.46 us -> 41.2 us
    pallas_call x0 -> x6, Pallas kernels: none -> 653 us  [the longest x5 359 us: logits_call(): pl.pallas_call(functools.partial(logits_kernel, cols), name='logits', gri...]
    dot_general x3 -> x5, matrix products: 890 us -> 322 us  [backward(): lax.dot_general(g, w, (((1,), (1,)), ((), ())), preferred_element_type=jn...]
    reduce_scatter x1 -> x5, waiting for transfers between devices: 432 us -> 0.06 us  [backward(): lax.psum_scatter(part, 'tp', scatter_dimension=0, tiled=True)]
    all_gather x1 -> x5, waiting for transfers between devices: 285 us -> 73.1 us  [gather(): return lax.all_gather(x, 'tp', axis=0, tiled=True)]
    psum x1 -> x0, waiting for transfers between devices: 43.6 us -> none  [local_step(): lax.psum(jnp.stack([jnp.sum(shifted, axis=-1), local_target]), 'tp')]
    reduce_sum x2 -> x5, other arithmetic: 41.5 us -> 2.53 us  [the longest x3 2.16 us: combine(): return (m, s, jnp.mean(m + jnp.log(s) - jnp.sum(t_all, axis=0)))]
    all_gather x1 -> x3, blocking collectives: 13.8 us -> 45.9 us  [the longest x2 31.7 us: combine(): lax.all_gather(jnp.concatenate(parts, axis=1), 'tp', axis=0, tiled=False)]
    convert_element_type x2 -> x10, other arithmetic: 71.2 us -> 103 us  [the longest x5 91.7 us: backward(): g = ((jnp.exp(z - m) / s - hit) / tokens).astype(jnp.bfloat16)]
  transfers between devices with their start and end apart: 3 -> 10, of which waited for: 3 -> 4; matrix products, arithmetic and copies ran while one was open for 16% -> 37% of each run, Pallas kernels for 0% -> 52%
where the time goes in v1:
time: 1270 us
  Pallas kernels  653 us (51%)
  matrix products  322 us (25%)
  other arithmetic  113 us (9%)
  waiting for transfers between devices  74.5 us (6%)
  blocking collectives  45.9 us (4%)
  local copies, waits for them, and re-layouts  41.2 us (3%)
  between operations  16.3 us (1%)
    pallas_call x5, Pallas kernels, logits_call(): pl.pallas_call(functools.partial(logits_kernel, cols), name='logits', gri...  359 us
    dot_general x5, matrix products, backward(): lax.dot_general(g, w, (((1,), (1,)), ((), ())), preferred_element_type=jn...  322 us
    pallas_call x1, Pallas kernels, wgrad_call(): pl.pallas_call(functools.partial(wgrad_kernel, len(xs)), name='wgrad', gr...  294 us
    convert_element_type x5, other arithmetic, backward(): g = ((jnp.exp(z - m) / s - hit) / tokens).astype(jnp.bfloat16)  91.7 us
    all_gather x5, waiting for transfers between devices, gather(): return lax.all_gather(x, 'tp', axis=0, tiled=True)  73.1 us
    all_gather x2, blocking collectives, combine(): lax.all_gather(jnp.concatenate(parts, axis=1), 'tp', axis=0, tiled=False)  31.7 us
  transfers between devices with their start and end apart: 10, of which 4 were waited for; matrix products, arithmetic and copies ran while one was open for 37% of the time, Pallas kernels for 52%

profile of v1, /device:TPU:0, one launch (start us, length us, event | category | flops | bytes accessed | tf_op | source)
XLA Modules:
  0.0 1265.9 jit_solution(14571394954373155688)
XLA Ops:
  7.2 3.1 fusion.8
  11.2 3.1 slice.133
  14.4 4.7 fusion.9
  19.8 14.3 %all-gather.3 = s32[8,2,512]{2,1,0:T(2,128)S(1)} all-gather(s32[1,2,512]{2,1,0:T(2,128)S(1)} %add_bitcast_fusion), channel_id=2, replica_groups=mesh['dp'=1,'tp'=8] {'tp'}, dimensions={0}, use_global_device_ids=true | all-gather | bytes 36864 | tf_op jit(solution)/shard_map/all_gather | solution.py:105
  37.4 1.4 copy.33
  38.8 23.6 %all-gather.12.cloned.1.call-done.x_ref.refs_0_ = bf16[1024,4096]{1,0:T(8,128)(2,1)} async-done(((bf16[128,4096]{1,0:T(8,128)(2,1)}), bf16[1024,4096]{1,0:T(8,128)(2,1)}) %all-gather.12.cloned.1.call-update) | async-done | bytes 8388624 | tf_op jit(solution)/shard_map/all_gather | solution.py:116
  62.4 46.3 %logits.5 = (f32[1024,4096]{1,0:T(8,128)}, f32[1024,128]{1,0:T(8,128)}, f32[1024,128]{1,0:T(8,128)}, f32[1024,128]{1,0:T(8,128)}) custom-call(bf16[1024,4096]{1,0:T(8,128)(2,1)} %all-gather.12.cloned.1.call-done.x_ref.refs_0_, bf16[4096,4096]{1,0:T(8,128)(2,1)} %w_ref.9, s32[1024,1]{1,0:T(8,128)} %copy.19.lab_ref), custom_call_target="tpu_custom_call" | custom-call | flops 34359738368 | bytes 58720256 | tf_op jit(solution)/shard_map/logits/pallas_call | solution.py:60
  108.7 3.9 all-gather.14.cloned.1.call-done.x_ref.refs_1_
  112.6 1.2 slice_reduce_fusion.14
  113.8 46.4 %logits.6 = (f32[1024,4096]{1,0:T(8,128)}, f32[1024,128]{1,0:T(8,128)}, f32[1024,128]{1,0:T(8,128)}, f32[1024,128]{1,0:T(8,128)}) custom-call(bf16[1024,4096]{1,0:T(8,128)(2,1)} %all-gather.14.cloned.1.call-done.x_ref.refs_1_, bf16[4096,4096]{1,0:T(8,128)(2,1)} %w_ref.9, s32[1024,1]{1,0:T(8,128)} %copy.20.lab_ref), custom_call_target="tpu_custom_call" | custom-call | flops 34359738368 | bytes 58720256 | tf_op jit(solution)/shard_map/logits/pallas_call | solution.py:60
  160.3 1.2 slice_reduce_fusion.11
  161.5 1.4 slice_reduce_fusion.12
  162.9 1.5 slice_reduce_fusion.9
  164.4 34.6 %all-gather.16.cloned.1.call-done.x_ref.refs_2_ = bf16[2048,4096]{1,0:T(8,128)(2,1)} async-done(((bf16[256,4096]{1,0:T(8,128)(2,1)}), bf16[2048,4096]{1,0:T(8,128)(2,1)}) %all-gather.16.cloned.1.call-update) | async-done | bytes 16777232 | tf_op jit(solution)/shard_map/all_gather | solution.py:116
  199.1 88.8 %logits.7 = (f32[2048,4096]{1,0:T(8,128)}, f32[2048,128]{1,0:T(8,128)}, f32[2048,128]{1,0:T(8,128)}, f32[2048,128]{1,0:T(8,128)}) custom-call(bf16[2048,4096]{1,0:T(8,128)(2,1)} %all-gather.16.cloned.1.call-done.x_ref.refs_2_, bf16[4096,4096]{1,0:T(8,128)(2,1)} %w_ref.9, s32[2048,1]{1,0:T(8,128)} %bitcast.92), custom_call_target="tpu_custom_call" | custom-call | flops 68719476736 | bytes 83886080 | tf_op jit(solution)/shard_map/logits/pallas_call | solution.py:60
  287.9 1.6 slice_reduce_fusion.8
  289.4 2.1 slice_reduce_fusion.6
  291.7 15.6 %all-gather.4 = f32[8,3,4096]{2,1,0:T(4,128)S(1)} all-gather(f32[1,3,4096]{2,1,0:T(4,128)S(1)} %maximum_bitcast_fusion), channel_id=3, replica_groups=mesh['dp'=1,'tp'=8] {'tp'}, dimensions={0}, use_global_device_ids=true | all-gather | bytes 442368 | tf_op jit(solution)/shard_map/all_gather | solution.py:126
  308.4 12.0 multiply_convert_fusion.4.refs_5_
  320.4 43.1 %fusion.15 = f32[1024,4096]{1,0:T(8,128)} fusion(bf16[1024,4096]{1,0:T(8,128)(2,1)} %multiply_convert_fusion.4.refs_5_, bf16[4096,4096]{1,0:T(8,128)(2,1)} %w_ref.9), kind=kOutput, calls=%fused_computation.63 | convolution fusion | flops 34359738368 | bytes 58720256 | tf_op jit(solution)/shard_map/dot_general | solution.py:139
  363.6 11.0 all-gather.20.cloned.1.call-done.x_ref.refs_4_
  374.6 12.0 multiply_convert_fusion.3.refs_6_
  386.6 43.1 %fusion.16 = f32[1024,4096]{1,0:T(8,128)} fusion(bf16[1024,4096]{1,0:T(8,128)(2,1)} %multiply_convert_fusion.3.refs_6_, bf16[4096,4096]{1,0:T(8,128)(2,1)} %w_ref.9), kind=kOutput, calls=%fused_computation.64 | convolution fusion | flops 34359738368 | bytes 58720256 | tf_op jit(solution)/shard_map/dot_general | solution.py:139
  430.5 22.6 %multiply_convert_fusion.2.refs_7_ = bf16[2048,4096]{1,0:T(8,128)(2,1)} fusion(f32[2048,4096]{1,0:T(8,128)} %get-tuple-element.50, s32[2048]{0:T(1024)S(1)} %bitcast.108, f32[2048]{0:T(1024)S(1)} %slice.175, f32[2048]{0:T(1024)S(1)} %slice.174), kind=kLoop, calls=%fused_computation.4 | loop fusion | flops 58720256 | bytes 50356224 | tf_op jit(solution)/shard_map/convert_element_type | solution.py:137
  453.1 78.6 %fusion.17 = f32[2048,4096]{1,0:T(8,128)} fusion(bf16[2048,4096]{1,0:T(8,128)(2,1)} %multiply_convert_fusion.2.refs_7_, bf16[4096,4096]{1,0:T(8,128)(2,1)} %w_ref.9), kind=kOutput, calls=%fused_computation.65 | convolution fusion | flops 68719476736 | bytes 83886080 | tf_op jit(solution)/shard_map/dot_general | solution.py:139
  532.4 1.3 copy.38
  533.7 1.3 copy.36
  535.1 88.7 %logits.8 = (f32[2048,4096]{1,0:T(8,128)}, f32[2048,128]{1,0:T(8,128)}, f32[2048,128]{1,0:T(8,128)}, f32[2048,128]{1,0:T(8,128)}) custom-call(bf16[2048,4096]{1,0:T(8,128)(2,1)} %all-gather.18.cloned.1.call-done.x_ref.refs_3_, bf16[4096,4096]{1,0:T(8,128)(2,1)} %w_ref.9, s32[2048,1]{1,0:T(8,128)} %bitcast.94), custom_call_target="tpu_custom_call" | custom-call | flops 68719476736 | bytes 83886080 | tf_op jit(solution)/shard_map/logits/pallas_call | solution.py:60
  623.8 1.6 slice_reduce_fusion.5
  625.4 1.6 slice_reduce_fusion.4
  627.0 1.6 slice_reduce_fusion.3
  628.6 88.5 %logits.9 = (f32[2048,4096]{1,0:T(8,128)}, f32[2048,128]{1,0:T(8,128)}, f32[2048,128]{1,0:T(8,128)}, f32[2048,128]{1,0:T(8,128)}) custom-call(bf16[2048,4096]{1,0:T(8,128)(2,1)} %all-gather.20.cloned.1.call-done.x_ref.refs_4_, bf16[4096,4096]{1,0:T(8,128)(2,1)} %w_ref.9, s32[2048,1]{1,0:T(8,128)} %bitcast.93), custom_call_target="tpu_custom_call" | custom-call | flops 68719476736 | bytes 83886080 | tf_op jit(solution)/shard_map/logits/pallas_call | solution.py:60
  717.1 1.6 slice_reduce_fusion.2
  718.6 1.6 slice_reduce_fusion.1
  720.2 1.6 slice_reduce_fusion
  721.8 16.1 %all-gather.5 = f32[8,3,4096]{2,1,0:T(4,128)S(1)} all-gather(f32[1,3,4096]{2,1,0:T(4,128)S(1)} %maximum_bitcast_fusion.1), channel_id=4, replica_groups=mesh['dp'=1,'tp'=8] {'tp'}, dimensions={0}, use_global_device_ids=true | all-gather | bytes 442368 | tf_op jit(solution)/shard_map/all_gather | solution.py:126
  740.7 22.5 %multiply_convert_fusion.1.refs_8_ = bf16[2048,4096]{1,0:T(8,128)(2,1)} fusion(f32[2048,4096]{1,0:T(8,128)} %get-tuple-element.61, s32[2048]{0:T(1024)S(1)} %bitcast.104, f32[2048]{0:T(1024)S(1)} %get-tuple-element.91, f32[2048]{0:T(1024)S(1)} %get-tuple-element.89), kind=kLoop, calls=%fused_computation.2 | loop fusion | flops 58720256 | bytes 50356224 | tf_op jit(solution)/shard_map/convert_element_type | solution.py:137
  763.2 78.5 %fusion.18 = f32[2048,4096]{1,0:T(8,128)} fusion(bf16[2048,4096]{1,0:T(8,128)(2,1)} %multiply_convert_fusion.1.refs_8_, bf16[4096,4096]{1,0:T(8,128)(2,1)} %w_ref.9), kind=kOutput, calls=%fused_computation.66 | convolution fusion | flops 68719476736 | bytes 83886080 | tf_op jit(solution)/shard_map/dot_general | solution.py:139
  842.5 22.6 %multiply_convert_fusion.refs_9_ = bf16[2048,4096]{1,0:T(8,128)(2,1)} fusion(f32[2048,4096]{1,0:T(8,128)} %get-tuple-element.62, s32[2048]{0:T(1024)S(1)} %bitcast.106, f32[2048]{0:T(1024)S(1)} %copy-done.13, f32[2048]{0:T(1024)S(1)} %copy-done.12), kind=kLoop, calls=%fused_computation | loop fusion | flops 58720256 | bytes 50356224 | tf_op jit(solution)/shard_map/convert_element_type | solution.py:137
  865.1 78.6 %fusion.19 = f32[2048,4096]{1,0:T(8,128)} fusion(bf16[2048,4096]{1,0:T(8,128)(2,1)} %multiply_convert_fusion.refs_9_, bf16[4096,4096]{1,0:T(8,128)(2,1)} %w_ref.9), kind=kOutput, calls=%fused_computation.67 | convolution fusion | flops 68719476736 | bytes 83886080 | tf_op jit(solution)/shard_map/dot_general | solution.py:139
  947.0 1.1 convert_element_type.55
  948.1 2.7 convert_element_type.56
  951.4 293.9 %wgrad.1 = bf16[4096,4096]{1,0:T(8,128)(2,1)} custom-call(bf16[1024,4096]{1,0:T(8,128)(2,1)} %all-gather.12.cloned.1.call-done.x_ref.refs_0_, bf16[1024,4096]{1,0:T(8,128)(2,1)} %all-gather.14.cloned.1.call-done.x_ref.refs_1_, bf16[2048,4096]{1,0:T(8,128)(2,1)} %all-gather.16.cloned.1.call-done.x_ref.refs_2_, ...), custom_call_target="tpu_custom_call" | custom-call | flops 274877906944 | bytes 167772160 | tf_op jit(solution)/shard_map/wgrad/pallas_call | solution.py:82
  1245.3 2.5 convert_element_type.57
  1247.8 3.4 pad_maximum_fusion
  1251.2 2.5 convert_element_type.58
  1253.7 2.5 convert_element_type.59
  1256.1 2.4 pad_maximum_fusion.1
  (97 shorter events, 13.6 us)
Async XLA Ops:
  7.2 12.6 copy-start.20
  7.2 12.6 copy-start.21
  7.2 55.2 %all-gather.12.cloned.1.call-start = ((), (), s32[]{:S(2)}) async-start(), calls=%async_computation.5 | async-start | bytes 9437184 | tf_op jit(solution)/shard_map/all_gather | solution.py:116
  10.4 102.2 %all-gather.14.cloned.1.call-start = ((), (), s32[]{:S(2)}) async-start(), calls=%async_computation.6 | async-start | bytes 9437184 | tf_op jit(solution)/shard_map/all_gather | solution.py:116
  11.1 187.9 %all-gather.16.cloned.1.call-start = ((), (), s32[]{:S(2)}) async-start(), calls=%async_computation.7 | async-start | bytes 18874368 | tf_op jit(solution)/shard_map/all_gather | solution.py:116
  14.3 349.3 %all-gather.18.cloned.1.call-start = ((), (), s32[]{:S(2)}) async-start(), calls=%async_computation.8 | async-start | bytes 18874368 | tf_op jit(solution)/shard_map/all_gather | solution.py:116
  19.1 355.5 %all-gather.20.cloned.1.call-start = ((), (), s32[]{:S(2)}) async-start(), calls=%async_computation.9 | async-start | bytes 18874368 | tf_op jit(solution)/shard_map/all_gather | solution.py:116
  19.7 608.8 %reduce-scatter.6.cloned.1.call-start = ((), (), s32[]{:S(2)}) async-start(), calls=%async_computation.10 | async-start | bytes 18874368 | tf_op jit(solution)/shard_map/reduce_scatter | solution.py:140
  113.8 47.7 %copy-start.1 = (f32[1024,128]{1,0:T(8,128)S(1)}, f32[1024,128]{1,0:T(8,128)}, u32[]{:S(2)}) copy-start(f32[1024,128]{1,0:T(8,128)} %get-tuple-element.35) | copy-start | bytes 1572868
  308.2 122.3 %copy-start.2 = (f32[4096]{0:T(1024)}, f32[4096]{0:T(1024)S(1)}, u32[]{:S(2)}) copy-start(f32[4096]{0:T(1024)S(1)} %get-tuple-element.65) | copy-start | bytes 49156
  308.4 122.1 %copy-start.6 = (f32[4096]{0:T(1024)}, f32[4096]{0:T(1024)S(1)}, u32[]{:S(2)}) copy-start(f32[4096]{0:T(1024)S(1)} %fusion.7) | copy-start | bytes 49156
  363.5 11.1 copy-start.19
  363.5 353.5 %reduce-scatter.8.cloned.1.call-start = ((), (), s32[]{:S(2)}) async-start(), calls=%async_computation.11 | async-start | bytes 18874368 | tf_op jit(solution)/shard_map/reduce_scatter | solution.py:140
  429.7 0.7 copy-start.18
  429.8 815.5 %reduce-scatter.10.cloned.1.call-start = ((), (), s32[]{:S(2)}) async-start(), calls=%async_computation.12 | async-start | bytes 37748736 | tf_op jit(solution)/shard_map/reduce_scatter | solution.py:140
  531.6 0.7 copy-start.17
  531.6 0.7 copy-start.16
  531.6 0.7 copy-start.15
  531.7 719.5 %reduce-scatter.12.cloned.1.call-start = ((), (), s32[]{:S(2)}) async-start(), calls=%async_computation.13 | async-start | bytes 37748736 | tf_op jit(solution)/shard_map/reduce_scatter | solution.py:140
  738.9 0.6 copy-start.4
  739.5 0.6 copy-start.8
  841.8 0.7 copy-start.14
  841.8 0.7 copy-start.12
  841.8 0.7 copy-start.13
  841.8 411.8 %reduce-scatter.14.cloned.1.call-start = ((), (), s32[]{:S(2)}) async-start(), calls=%async_computation.14 | async-start | bytes 37748736 | tf_op jit(solution)/shard_map/reduce_scatter | solution.py:140
  943.7 0.7 copy-start.3
  943.7 0.7 copy-start.7
  943.7 0.7 copy-start.10
  943.7 2.0 copy-start.5
  943.7 2.0 copy-start.9
  943.7 2.0 copy-start.11
  943.7 3.3 copy-start
Sparse Core Ops, SparseCore 0:
  10.5 51.8 all-gather.11
  64.2 48.3 all-gather.13
  115.0 84.0 all-gather.15
  201.3 84.0 all-gather.17
  287.7 86.8 all-gather.19
  377.9 106.9 reduce-scatter.5
  488.4 106.9 reduce-scatter.7
  598.9 199.4 reduce-scatter.9
  841.9 196.2 reduce-scatter.11
  1041.5 196.2 reduce-scatter.13

commit v2 on v1

--- a/solution.py
+++ b/solution.py
@@ -7,11 +7,11 @@
 from jax.experimental.pallas import tpu as pltpu
 from jax.sharding import PartitionSpec as P
 
-PIECES = ((0, 128), (0, 128), (0, 256), (1, 256), (1, 256))
+PIECES = ((0, 192), (0, 192), (0, 128), (1, 256), (1, 256))
 LANES = 128
 
 
-def logits_kernel(cols, x_ref, w_ref, lab_ref, z_ref, m_ref, s_ref, t_ref, m_acc, s_acc, t_acc):
+def logits_kernel(cols, x_ref, w_ref, lab_ref, z_ref, st_ref, m_acc, s_acc, t_acc):
     v = pl.program_id(0)
     rows, tile = x_ref.shape[0], 512
 
@@ -47,9 +47,8 @@
         m = jnp.max(m_acc[...], axis=1, keepdims=True)
         s = jnp.sum(s_acc[...] * jnp.exp(m_acc[...] - m), axis=1, keepdims=True)
         t = jnp.sum(t_acc[...], axis=1, keepdims=True)
-        m_ref[...] = jnp.broadcast_to(m, m_ref.shape)
-        s_ref[...] = jnp.broadcast_to(s, s_ref.shape)
-        t_ref[...] = jnp.broadcast_to(t, t_ref.shape)
+        lane = lax.broadcasted_iota(jnp.int32, st_ref.shape, 1)
+        st_ref[...] = jnp.where(lane == 0, m, jnp.where(lane == 1, s, t))
 
 
 def logits_call(x, w, lab, cols=512):
@@ -61,8 +60,8 @@
         functools.partial(logits_kernel, cols), name="logits",
         grid=(vocab // cols,),
         in_specs=[pl.BlockSpec((rows, hidden), lambda v: (0, 0)), pl.BlockSpec((hidden, cols), lambda v: (0, v)), pl.BlockSpec((rows, 1), lambda v: (0, 0))],
-        out_specs=[pl.BlockSpec((rows, cols), lambda v: (0, v)), stat_spec, stat_spec, stat_spec],
-        out_shape=[jax.ShapeDtypeStruct((rows, vocab), jnp.float32), stat, stat, stat],
+        out_specs=[pl.BlockSpec((rows, cols), lambda v: (0, v)), stat_spec],
+        out_shape=[jax.ShapeDtypeStruct((rows, vocab), jnp.float32), stat],
         scratch_shapes=[pltpu.VMEM((rows, LANES), jnp.float32)] * 3,
         compiler_params=pltpu.CompilerParams(vmem_limit_bytes=63 << 20, dimension_semantics=("arbitrary",)),
         cost_estimate=pl.CostEstimate(flops=2 * rows * hidden * vocab, bytes_accessed=(rows + vocab) * hidden * 2 + rows * vocab * 4, transcendentals=rows * vocab),
@@ -119,8 +118,8 @@
 
         def forward(i, x, token=None):
             x = x if token is None else after(x, token)
-            z, m, s, t = logits_call(x, w, labs[i])
-            return z, jnp.stack([m[:, 0], s[:, 0], t[:, 0]])
+            z, st = logits_call(x, w, labs[i])
+            return z, st[:, :3].T
 
         def combine(parts):
             every = lax.all_gather(jnp.concatenate(parts, axis=1), "tp", axis=0, tiled=False)
@@ -145,8 +144,8 @@
         z2, st2 = forward(2, gx[2], z1)
         stat_a = combine([st0, st1, st2])
         b0 = backward(0, z0, stat_a, z2)
-        b1 = backward(1, z1, stat_a, (b0[1], gx[3], gx[4]))
-        b2 = backward(2, z2, stat_a, b1[1])
+        b1 = backward(1, z1, stat_a, b0[1])
+        b2 = backward(2, z2, stat_a, (b1[1], gx[3], gx[4]))
         z3, st3 = forward(3, gx[3], b2[1])
         z4, st4 = forward(4, gx[4], (z3, b0[2]))
         stat_b = combine([st3, st4])

time: 1270 us -> 1230 us (0.969)
  waiting for transfers between devices: 74.5 us -> 43.5 us
    all_gather x5, waiting for transfers between devices: 73.1 us -> 42 us  [gather(): return lax.all_gather(x, 'tp', axis=0, tiled=True)]
    slice x12 -> x1, local copies, waits for them, and re-layouts: 18.5 us -> 0.07 us  [local_step(): labels[:, mb, s0:s0 + size].reshape(-1, 1)]
  transfers between devices with their start and end apart: 10 -> 10, of which waited for: 4 -> 1; matrix products, arithmetic and copies ran while one was open for 37% -> 37% of each run, Pallas kernels for 52% -> 53%
where the time goes in v2:
time: 1230 us; the launch traced here: 1220 us
  Pallas kernels  650 us (53%)
  matrix products  326 us (27%)
  other arithmetic  111 us (9%)
  waiting for transfers between devices  43.5 us (4%)
  blocking collectives  42.9 us (3%)
  local copies, waits for them, and re-layouts  33.2 us (3%)
  between operations  16.1 us (1%)
    pallas_call x5, Pallas kernels, logits_call(): pl.pallas_call(functools.partial(logits_kernel, cols), name='logits', gri...  356 us
    dot_general x5, matrix products, backward(): lax.dot_general(g, w, (((1,), (1,)), ((), ())), preferred_element_type=jn...  326 us
    pallas_call x1, Pallas kernels, wgrad_call(): pl.pallas_call(functools.partial(wgrad_kernel, len(xs)), name='wgrad', gr...  294 us
    convert_element_type x5, other arithmetic, backward(): g = ((jnp.exp(z - m) / s - hit) / tokens).astype(jnp.bfloat16)  91.4 us
    all_gather x5, waiting for transfers between devices, gather(): return lax.all_gather(x, 'tp', axis=0, tiled=True)  42 us
    all_gather x2, blocking collectives, combine(): lax.all_gather(jnp.concatenate(parts, axis=1), 'tp', axis=0, tiled=False)  28.4 us
  transfers between devices with their start and end apart: 10, of which 1 were waited for; matrix products, arithmetic and copies ran while one was open for 37% of the time, Pallas kernels for 53%

profile of v2, /device:TPU:0, one launch (start us, length us, event | category | flops | bytes accessed | tf_op | source)
XLA Modules:
  0.0 1222.4 jit_solution(10051542035459454274)
XLA Ops:
  7.2 3.9 fusion.8
  11.2 0.7 all-gather.14.cloned.1.call-update
  12.0 2.3 slice.99
  14.4 4.7 fusion.9
  19.8 14.5 %all-gather.3 = s32[8,2,512]{2,1,0:T(2,128)S(1)} all-gather(s32[1,2,512]{2,1,0:T(2,128)S(1)} %add_bitcast_fusion), channel_id=2, replica_groups=mesh['dp'=1,'tp'=8] {'tp'}, dimensions={0}, use_global_device_ids=true | all-gather | bytes 36864 | tf_op jit(solution)/shard_map/all_gather | solution.py:104
  35.1 1.5 reshape_squeeze.20.lab_ref
  36.6 1.0 copy.24.lab_ref
  37.6 1.5 reshape_squeeze.21.lab_ref
  39.1 42.0 %all-gather.12.cloned.1.call-done.x_ref.refs_0_ = bf16[1536,4096]{1,0:T(8,128)(2,1)} async-done(((bf16[192,4096]{1,0:T(8,128)(2,1)}), bf16[1536,4096]{1,0:T(8,128)(2,1)}) %all-gather.12.cloned.1.call-update) | async-done | bytes 12582928 | tf_op jit(solution)/shard_map/all_gather | solution.py:115
  81.1 66.9 %logits.5 = (f32[1536,4096]{1,0:T(8,128)}, f32[1536,128]{1,0:T(8,128)}) custom-call(bf16[1536,4096]{1,0:T(8,128)(2,1)} %all-gather.12.cloned.1.call-done.x_ref.refs_0_, bf16[4096,4096]{1,0:T(8,128)(2,1)} %w_ref.9, s32[1536,1]{1,0:T(8,128)} %reshape_squeeze.20.lab_ref), custom_call_target="tpu_custom_call" | custom-call | flops 51539607552 | bytes 71303168 | tf_op jit(solution)/shard_map/logits/pallas_call | solution.py:59
  148.0 1.2 slice_bitcast_fusion.3
  149.5 66.8 %logits.6 = (f32[1536,4096]{1,0:T(8,128)}, f32[1536,128]{1,0:T(8,128)}) custom-call(bf16[1536,4096]{1,0:T(8,128)(2,1)} %all-gather.14.cloned.1.call-done.x_ref.refs_1_, bf16[4096,4096]{1,0:T(8,128)(2,1)} %w_ref.9, s32[1536,1]{1,0:T(8,128)} %reshape_squeeze.21.lab_ref), custom_call_target="tpu_custom_call" | custom-call | flops 51539607552 | bytes 71303168 | tf_op jit(solution)/shard_map/logits/pallas_call | solution.py:59
  216.3 1.2 slice_bitcast_fusion.2
  217.7 46.3 %logits.7 = (f32[1024,4096]{1,0:T(8,128)}, f32[1024,128]{1,0:T(8,128)}) custom-call(bf16[1024,4096]{1,0:T(8,128)(2,1)} %all-gather.16.cloned.1.call-done.x_ref.refs_2_, bf16[4096,4096]{1,0:T(8,128)(2,1)} %w_ref.9, s32[1024,1]{1,0:T(8,128)} %copy.24.lab_ref), custom_call_target="tpu_custom_call" | custom-call | flops 34359738368 | bytes 58720256 | tf_op jit(solution)/shard_map/logits/pallas_call | solution.py:59
  264.1 1.1 slice_bitcast_fusion.4
  265.4 16.1 %all-gather.4 = f32[8,3,4096]{2,1,0:T(4,128)S(1)} all-gather(f32[1,3,4096]{2,1,0:T(4,128)S(1)} %maximum_bitcast_fusion), channel_id=3, replica_groups=mesh['dp'=1,'tp'=8] {'tp'}, dimensions={0}, use_global_device_ids=true | all-gather | bytes 442368 | tf_op jit(solution)/shard_map/all_gather | solution.py:125
  281.5 0.9 slice_reduce_fusion.1
  283.6 17.1 %multiply_convert_fusion.3.refs_5_ = bf16[1536,4096]{1,0:T(8,128)(2,1)} fusion(f32[1536,4096]{1,0:T(8,128)} %get-tuple-element.32, s32[1536]{0:T(1024)S(1)} %eq.76, f32[1536]{0:T(1024)S(1)} %get-tuple-element.74, f32[1536]{0:T(1024)S(1)} %get-tuple-element.71), kind=kLoop, calls=%fused_computation.6 | loop fusion | flops 44040192 | bytes 37767168 | tf_op jit(solution)/shard_map/convert_element_type | solution.py:136
  300.8 62.7 %fusion.16 = f32[1536,4096]{1,0:T(8,128)} fusion(bf16[1536,4096]{1,0:T(8,128)(2,1)} %multiply_convert_fusion.3.refs_5_, bf16[4096,4096]{1,0:T(8,128)(2,1)} %w_ref.9), kind=kOutput, calls=%fused_computation.53 | convolution fusion | flops 51539607552 | bytes 71303168 | tf_op jit(solution)/shard_map/dot_general | solution.py:138
  363.5 0.6 copy-done.11
  364.2 17.1 %multiply_convert_fusion.2.refs_6_ = bf16[1536,4096]{1,0:T(8,128)(2,1)} fusion(f32[1536,4096]{1,0:T(8,128)} %get-tuple-element.33, s32[1536]{0:T(1024)S(1)} %eq.80, f32[1536]{0:T(1024)S(1)} %get-tuple-element.75, f32[1536]{0:T(1024)S(1)} %get-tuple-element.70), kind=kLoop, calls=%fused_computation.4 | loop fusion | flops 44040192 | bytes 37767168 | tf_op jit(solution)/shard_map/convert_element_type | solution.py:136
  381.3 62.9 %fusion.17 = f32[1536,4096]{1,0:T(8,128)} fusion(bf16[1536,4096]{1,0:T(8,128)(2,1)} %multiply_convert_fusion.2.refs_6_, bf16[4096,4096]{1,0:T(8,128)(2,1)} %w_ref.9), kind=kOutput, calls=%fused_computation.54 | convolution fusion | flops 51539607552 | bytes 71303168 | tf_op jit(solution)/shard_map/dot_general | solution.py:138
  444.3 0.7 copy-done.7
  446.2 1.4 copy.45
  447.6 1.3 copy.43
  448.9 0.7 slice.134
  449.6 12.1 multiply_convert_fusion.4.refs_7_
  461.7 43.1 %fusion.18 = f32[1024,4096]{1,0:T(8,128)} fusion(bf16[1024,4096]{1,0:T(8,128)(2,1)} %multiply_convert_fusion.4.refs_7_, bf16[4096,4096]{1,0:T(8,128)(2,1)} %w_ref.9), kind=kOutput, calls=%fused_computation.55 | convolution fusion | flops 34359738368 | bytes 58720256 | tf_op jit(solution)/shard_map/dot_general | solution.py:138
  504.9 88.0 %logits.8 = (f32[2048,4096]{1,0:T(8,128)}, f32[2048,128]{1,0:T(8,128)}) custom-call(bf16[2048,4096]{1,0:T(8,128)(2,1)} %all-gather.18.cloned.1.call-done.x_ref.refs_3_, bf16[4096,4096]{1,0:T(8,128)(2,1)} %w_ref.9, s32[2048,1]{1,0:T(8,128)} %bitcast.88), custom_call_target="tpu_custom_call" | custom-call | flops 68719476736 | bytes 83886080 | tf_op jit(solution)/shard_map/logits/pallas_call | solution.py:59
  592.8 1.3 slice_bitcast_fusion.1
  594.5 87.7 %logits.9 = (f32[2048,4096]{1,0:T(8,128)}, f32[2048,128]{1,0:T(8,128)}) custom-call(bf16[2048,4096]{1,0:T(8,128)(2,1)} %all-gather.20.cloned.1.call-done.x_ref.refs_4_, bf16[4096,4096]{1,0:T(8,128)(2,1)} %w_ref.9, s32[2048,1]{1,0:T(8,128)} %bitcast.87), custom_call_target="tpu_custom_call" | custom-call | flops 68719476736 | bytes 83886080 | tf_op jit(solution)/shard_map/logits/pallas_call | solution.py:59
  682.2 1.3 slice_bitcast_fusion
  683.9 12.3 %all-gather.5 = f32[8,3,4096]{2,1,0:T(4,128)S(1)} all-gather(f32[1,3,4096]{2,1,0:T(4,128)S(1)} %maximum_bitcast_fusion.1), channel_id=4, replica_groups=mesh['dp'=1,'tp'=8] {'tp'}, dimensions={0}, use_global_device_ids=true | all-gather | bytes 442368 | tf_op jit(solution)/shard_map/all_gather | solution.py:125
  696.2 1.0 fusion.10
  699.0 22.5 %multiply_convert_fusion.1.refs_8_ = bf16[2048,4096]{1,0:T(8,128)(2,1)} fusion(f32[2048,4096]{1,0:T(8,128)} %get-tuple-element.41, s32[2048]{0:T(1024)S(1)} %bitcast.89, f32[2048]{0:T(1024)S(1)} %get-tuple-element.69, f32[2048]{0:T(1024)S(1)} %get-tuple-element.67), kind=kLoop, calls=%fused_computation.2 | loop fusion | flops 58720256 | bytes 50356224 | tf_op jit(solution)/shard_map/convert_element_type | solution.py:136
  721.5 78.5 %fusion.19 = f32[2048,4096]{1,0:T(8,128)} fusion(bf16[2048,4096]{1,0:T(8,128)(2,1)} %multiply_convert_fusion.1.refs_8_, bf16[4096,4096]{1,0:T(8,128)(2,1)} %w_ref.9), kind=kOutput, calls=%fused_computation.56 | convolution fusion | flops 68719476736 | bytes 83886080 | tf_op jit(solution)/shard_map/dot_general | solution.py:138
  800.1 0.6 copy-done.17
  800.8 22.6 %multiply_convert_fusion.refs_9_ = bf16[2048,4096]{1,0:T(8,128)(2,1)} fusion(f32[2048,4096]{1,0:T(8,128)} %get-tuple-element.42, s32[2048]{0:T(1024)S(1)} %bitcast.90, f32[2048]{0:T(1024)S(1)} %copy-done.16, f32[2048]{0:T(1024)S(1)} %copy-done.15), kind=kLoop, calls=%fused_computation | loop fusion | flops 58720256 | bytes 50356224 | tf_op jit(solution)/shard_map/convert_element_type | solution.py:136
  823.3 78.6 %fusion.20 = f32[2048,4096]{1,0:T(8,128)} fusion(bf16[2048,4096]{1,0:T(8,128)(2,1)} %multiply_convert_fusion.refs_9_, bf16[4096,4096]{1,0:T(8,128)(2,1)} %w_ref.9), kind=kOutput, calls=%fused_computation.57 | convolution fusion | flops 68719476736 | bytes 83886080 | tf_op jit(solution)/shard_map/dot_general | solution.py:138
  902.0 0.6 copy-done.1
  904.0 1.7 convert_element_type.57
  907.0 2.1 convert_element_type.55
  909.1 2.1 convert_element_type.56
  911.7 2.1 pad_maximum_fusion
  913.9 294.0 %wgrad.1 = bf16[4096,4096]{1,0:T(8,128)(2,1)} custom-call(bf16[1536,4096]{1,0:T(8,128)(2,1)} %all-gather.12.cloned.1.call-done.x_ref.refs_0_, bf16[1536,4096]{1,0:T(8,128)(2,1)} %all-gather.14.cloned.1.call-done.x_ref.refs_1_, bf16[1024,4096]{1,0:T(8,128)(2,1)} %all-gather.16.cloned.1.call-done.x_ref.refs_2_, ...), custom_call_target="tpu_custom_call" | custom-call | flops 274877906944 | bytes 167772160 | tf_op jit(solution)/shard_map/wgrad/pallas_call | solution.py:81
  1207.9 2.5 convert_element_type.58
  1210.4 2.5 convert_element_type.59
  1212.8 2.4 pad_maximum_fusion.1
  (94 shorter events, 9.5 us)
Async XLA Ops:
  7.2 12.6 %copy-start.19 = (s32[512]{0:T(512)S(1)}, s32[512]{0:T(512)}, u32[]{:S(2)}) copy-start(s32[512]{0:T(512)} %param.8) | copy-start | bytes 6148
  7.2 12.6 %copy-start.20 = (s32[512]{0:T(512)S(1)}, s32[512]{0:T(512)}, u32[]{:S(2)}) copy-start(s32[512]{0:T(512)} %param.7) | copy-start | bytes 6148
  7.2 74.0 %all-gather.12.cloned.1.call-start = ((), (), s32[]{:S(2)}) async-start(), calls=%async_computation.5 | async-start | bytes 14155776 | tf_op jit(solution)/shard_map/all_gather | solution.py:115
  11.2 138.3 %all-gather.14.cloned.1.call-start = ((), (), s32[]{:S(2)}) async-start(), calls=%async_computation.6 | async-start | bytes 14155776 | tf_op jit(solution)/shard_map/all_gather | solution.py:115
  11.9 205.8 %all-gather.16.cloned.1.call-start = ((), (), s32[]{:S(2)}) async-start(), calls=%async_computation.7 | async-start | bytes 9437184 | tf_op jit(solution)/shard_map/all_gather | solution.py:115
  14.3 435.3 %all-gather.18.cloned.1.call-start = ((), (), s32[]{:S(2)}) async-start(), calls=%async_computation.8 | async-start | bytes 18874368 | tf_op jit(solution)/shard_map/all_gather | solution.py:115
  19.1 430.5 %all-gather.20.cloned.1.call-start = ((), (), s32[]{:S(2)}) async-start(), calls=%async_computation.9 | async-start | bytes 18874368 | tf_op jit(solution)/shard_map/all_gather | solution.py:115
  19.7 574.7 %reduce-scatter.6.cloned.1.call-start = ((), (), s32[]{:S(2)}) async-start(), calls=%async_computation.10 | async-start | bytes 28311552 | tf_op jit(solution)/shard_map/reduce_scatter | solution.py:139
  34.3 0.6 copy-start.6
  35.0 2.6 copy-start.10
  282.4 0.6 copy-start
  283.0 0.6 copy-start.4
  363.5 0.7 copy-start.11
  363.5 320.4 %reduce-scatter.8.cloned.1.call-start = ((), (), s32[]{:S(2)}) async-start(), calls=%async_computation.11 | async-start | bytes 28311552 | tf_op jit(solution)/shard_map/reduce_scatter | solution.py:139
  444.2 0.8 copy-start.7
  444.2 5.4 slice-start
  444.2 5.4 copy-start.18
  444.2 459.7 %reduce-scatter.10.cloned.1.call-start = ((), (), s32[]{:S(2)}) async-start(), calls=%async_computation.12 | async-start | bytes 18874368 | tf_op jit(solution)/shard_map/reduce_scatter | solution.py:139
  504.8 703.0 %reduce-scatter.12.cloned.1.call-start = ((), (), s32[]{:S(2)}) async-start(), calls=%async_computation.13 | async-start | bytes 37748736 | tf_op jit(solution)/shard_map/reduce_scatter | solution.py:139
  594.5 104.5 %copy-start.14 = (s32[1,2,8,128]{3,1,2,0:T(2,128)S(1)}, s32[1,2,8,128]{3,1,2,0:T(2,128)}, u32[]{:S(2)}) copy-start(s32[1,2,8,128]{3,1,2,0:T(2,128)} %copy.46) | copy-start | bytes 24580
  697.2 0.6 copy-start.2
  697.8 0.6 copy-start.8
  800.0 0.7 copy-start.17
  800.0 0.7 copy-start.15
  800.1 0.7 copy-start.16
  800.1 410.3 %reduce-scatter.14.cloned.1.call-start = ((), (), s32[]{:S(2)}) async-start(), calls=%async_computation.14 | async-start | bytes 37748736 | tf_op jit(solution)/shard_map/reduce_scatter | solution.py:139
  901.9 0.7 copy-start.1
  901.9 0.7 copy-start.5
  901.9 0.7 copy-start.12
  901.9 3.8 copy-start.3
  901.9 3.8 copy-start.9
  901.9 3.8 copy-start.13
Sparse Core Ops, SparseCore 0:
  11.3 69.7 all-gather.11
  83.0 66.2 all-gather.13
  151.1 48.3 all-gather.15
  201.7 87.2 all-gather.17
  291.2 84.0 all-gather.19
  378.7 146.4 reduce-scatter.5
  528.8 146.4 reduce-scatter.7
  678.8 106.9 reduce-scatter.9
  800.2 196.2 reduce-scatter.11
  999.8 196.2 reduce-scatter.13
